TPU v7x, 32 devices: a whole 2x2x4 slice. The times are simulated.
32 devices in a mesh: dp: 4 (over z), mp: 8 (over y, x, core).
Axes of the slice: x: 2, y: 2, z: 4, core: 2. Of those that a mesh axis runs over, the one named last changes fastest.
Arguments:
- weight: bfloat16 [5120, 32768], P('dp', 'mp'), may hold values from -0.078125 to 0.078125
- rank_map: int32 [8], replicated, may hold values from 0 to 7, each once
Outputs:
- quant_out: bfloat16 [5120, 32768], P(None, 'mp')
- scale_out: bfloat16 [5120, 256], P(None, 'mp')
- checksum: float32 [256], replicated
Inputs may be any that keep to these rules, and one draw needn't show every extreme that they name: `rank_map`: a permutation of 0 to 7.
All inputs are finite; a program needn't handle non-finite values.
Results may differ from a plain program's by a relative error of at most 0.0085.
Values may be sent and summed in bfloat16 or wider, within the bound.
A program may use at most 192 MiB of HBM per device.

v0:
```python
import math

import jax
import jax.numpy as jnp
from jax import lax
from jax.sharding import PartitionSpec as P

D = 5120


floor_ratio = 0.25


def quantize(weight):
    rows, cols = weight.shape
    blocks = weight.astype(jnp.float32).reshape(rows, cols // 128, 128)
    peak = jnp.max(jnp.abs(blocks), axis=2)
    scale = (jnp.maximum(peak, floor_ratio / math.sqrt(D)) / 127.0).astype(jnp.bfloat16)
    quant = (blocks / scale.astype(jnp.float32)[:, :, None]).astype(jnp.bfloat16)
    return (quant.reshape(rows, cols), scale)


def inverse(rank_map):
    count = rank_map.shape[0]
    ids = jnp.arange(count)
    match = (rank_map[None, :] == ids[:, None]).astype(jnp.int32)
    return jnp.sum(ids[None, :] * match, axis=1)


def arrange(quant, scale, inv, count):
    rows, nblocks = scale.shape
    group = nblocks // count
    grouped = jnp.take(quant.reshape(rows, group, count, 128), inv, axis=2)
    scales = jnp.take(scale.reshape(rows, group, count), inv, axis=2)
    return (grouped, scales)


def settle(quant, scale):
    rows = quant.shape[0]
    return (quant.reshape(rows, -1), scale.reshape(rows, -1))


def local(weight, rank_map):
    count = lax.axis_size("mp")
    rank = lax.axis_index("mp")
    inv = inverse(rank_map)
    quant, scale = quantize(weight)
    grouped, scales = arrange(quant, scale, inv, count)
    moved_quant, moved_scale = (
        lax.all_to_all(grouped, "mp", split_axis=2, concat_axis=1, tiled=True),
        lax.all_to_all(scales, "mp", split_axis=2, concat_axis=1, tiled=True),
    )
    local_quant, local_scale = settle(moved_quant, moved_scale)
    quant_out, scale_out = (
        lax.all_gather(local_quant, "dp", axis=0, tiled=True),
        lax.all_gather(local_scale, "dp", axis=0, tiled=True),
    )
    divisor = 127.0 * math.sqrt(D * 128)
    rows, nblocks = scale.shape
    partial_value = jnp.sum(quant.reshape(rows, nblocks, 128), axis=(0, 2), dtype=jnp.float32)
    whole = jnp.zeros((nblocks * count,), jnp.float32)
    whole = lax.dynamic_update_slice_in_dim(whole, partial_value, rank * nblocks, 0)
    totals = lax.psum(whole, ("dp", "mp"))
    return (quant_out, scale_out, totals / divisor)


def solution(mesh):
    in_specs = (P("dp", "mp"), P())
    out_specs = (P(None, "mp"), P(None, "mp"), P())
    return jax.shard_map(local, mesh=mesh, in_specs=in_specs, out_specs=out_specs, check_vma=False)
```

profile of v0, /device:TPU:0, one launch (start us, length us, event | category | flops | bytes accessed | tf_op | source)
XLA Modules:
  0.0 934.2 jit_solution(3376004744070620664)
XLA Ops:
  7.2 0.0 all-gather.2.cloned.1.call-start
  7.2 0.8 select_reduce_fusion
  8.0 15.1 %copy.14 = bf16[1280,4096]{0,1:T(8,128)(2,1)} copy(bf16[1280,4096]{1,0:T(8,128)(2,1)} %param.2) | data formatting | bytes 20971520 | tf_op args[0]
  23.1 6.4 bitcast_reduce_fusion
  29.6 0.5 copy-done
  30.0 6.1 fusion.1
  36.2 9.5 %gather_fusion = bf16[8,1280,4,128]{1,3,2,0:T(8,128)(2,1)} fusion(bf16[1280,4,8,128]{0,3,1,2:T(8,128)(2,1)} %fusion.1, s32[1024]{0:T(1024)S(1)} %pad_clamp_fusion), kind=kCustom, calls=%fused_computation | custom fusion | bytes 20971552 | tf_op jit(solution)/shard_map/jit(_take)/gather | solution.py:33
  45.6 8.9 select_bitcast_fusion
  54.5 123.3 %all_to_all.30 = bf16[1280,4,8,128]{0,3,1,2:T(8,128)(2,1)} all-to-all(bf16[1280,4,8,128]{0,3,1,2:T(8,128)(2,1)} %select_bitcast_fusion), channel_id=1, replica_groups=mesh['dp'=4,'mp'=8] {'mp'}, dimensions={2} | all-to-all | bytes 20971520 | tf_op jit(solution)/shard_map/all_to_all | solution.py:50
  177.8 14.3 %copy.17 = bf16[1280,4096]{1,0:T(8,128)(2,1)} copy(bf16[1280,4096]{0,1:T(8,128)(2,1)} %bitcast.33) | data formatting | bytes 20971520 | tf_op jit(solution)/shard_map/reshape | solution.py:40
  192.1 0.0 all-gather.2.cloned.1.call-update
  192.2 0.6 gather_fusion.1
  192.8 0.7 select_bitcast_fusion.1
  193.6 3.4 all-to-all-start.1
  196.9 8.0 convert_reduce_fusion
  204.9 0.1 bitcast_reduce_fusion.1
  205.0 0.2 dynamic_update_slice.3
  205.3 80.7 %psum.7 = f32[256]{0:T(256)S(1)} all-reduce(f32[256]{0:T(256)S(1)} %dynamic_update_slice.3), channel_id=1, replica_groups=mesh['dp'=4,'mp'=8] {'dp','mp'}, use_global_device_ids=true, to_apply=%region_4.5 | all-reduce | flops 256 | bytes 2048 | tf_op jit(solution)/shard_map/psum | solution.py:63
  285.9 0.6 broadcast_multiply_fusion
  286.5 0.0 all-to-all-done.1
  286.5 50.5 %all_gather.7 = bf16[5120,32]{0,1:T(8,128)(2,1)S(1)} all-gather(bf16[1280,32]{0,1:T(8,128)(2,1)S(1)} %reshape.58), channel_id=1, replica_groups=mesh['dp'=4,'mp'=8] {'dp'}, dimensions={0}, use_global_device_ids=true | all-gather | bytes 409600 | tf_op jit(solution)/shard_map/all_gather | solution.py:56
  337.1 561.4 %all-gather.2.cloned.1.call-done = bf16[5120,4096]{1,0:T(8,128)(2,1)} async-done(((bf16[1280,4096]{1,0:T(8,128)(2,1)}), bf16[5120,4096]{1,0:T(8,128)(2,1)}) %all-gather.2.cloned.1.call-update) | async-done | bytes 41943056 | tf_op jit(solution)/shard_map/all_gather | solution.py:55
  898.5 28.2 %copy.25 = bf16[5120,4096]{1,0:T(8,128)(2,1)} copy(bf16[5120,4096]{1,0:T(8,128)(2,1)} %all-gather.2.cloned.1.call-done) | data formatting | bytes 83886080
  926.6 0.7 copy.26
  (9 shorter events, 0.1 us)
Async XLA Ops:
  7.2 891.3 %all-gather.2.cloned.1.call-start = ((), (), s32[]{:S(2)}) async-start(), calls=%async_computation.2 | async-start | bytes 52428800 | tf_op jit(solution)/shard_map/all_gather | solution.py:55
  23.1 7.0 copy-start
  193.6 92.9 %all-to-all-start.1 = ((bf16[1280,4,8]{0,1,2:T(4,128)(2,1)}), bf16[1280,4,8]{0,1,2:T(4,128)(2,1)S(1)}, u32[]{:S(2)}, u32[]{:S(2)}) async-start(bf16[1280,4,8]{0,1,2:T(4,128)(2,1)} %select_bitcast_fusion.1), calls=%async_computation.1 | async-start | bytes 163840 | tf_op jit(solution)/shard_map/all_to_all | solution.py:51
Sparse Core Ops, SparseCore 0:
  192.3 706.1 all-gather.1
where the time goes:
time: 935 us; the launch traced here: 934 us
  waiting for transfers between devices  561 us (60%)
  blocking collectives  255 us (27%)
  local copies, waits for them, and re-layouts  69.1 us (7%)
  other arithmetic  31.6 us (3%)
  between operations  14.1 us (2%)
    all_gather x1, waiting for transfers between devices, local(): lax.all_gather(local_quant, 'dp', axis=0, tiled=True)  561 us
    all_to_all x1, blocking collectives, local(): lax.all_to_all(grouped, 'mp', split_axis=2, concat_axis=1, tiled=True)  123 us
    psum x1, blocking collectives, local(): totals = lax.psum(whole, ('dp', 'mp'))  80.7 us
    all_gather x1, blocking collectives, local(): lax.all_gather(local_scale, 'dp', axis=0, tiled=True)  50.5 us
    unnamed x5, local copies, waits for them, and re-layouts  44.4 us
  transfers between devices with their start and end apart: 2, of which 1 were waited for; matrix products, arithmetic and copies ran while one was open for 1% of the time, Pallas kernels for 0%

commit v1 on v0

v1 whole, which is shorter than its diff:
```python
import functools
import math

import jax
import jax.numpy as jnp
from jax import lax
from jax.experimental import pallas as pl
from jax.experimental.pallas import tpu as pltpu
from jax.sharding import PartitionSpec as P

LANES = 128
FLOOR_RATIO = 0.25
CHUNKS = 2
MESH = pl.DeviceIdType.MESH


def inverse(rank_map):
    count = rank_map.shape[0]
    ids = jnp.arange(count, dtype=jnp.int32)
    match = (rank_map[None, :] == ids[:, None]).astype(jnp.int32)
    return jnp.sum(ids[None, :] * match, axis=1).astype(jnp.int32)


def quantize_kernel(floor, count, group, inv_ref, w_ref, q_ref, s_ref, p_ref, acc_ref):
    step = pl.program_id(0)
    tile = w_ref.shape[0]
    nblocks = count * group

    @pl.when(step == 0)
    def _():
        acc_ref[...] = jnp.zeros_like(acc_ref)

    lane = lax.broadcasted_iota(jnp.int32, (tile, LANES), 1)
    scales = jnp.zeros((tile, LANES), jnp.float32)
    for r in range(count):
        for i in range(group):
            b = i * count + inv_ref[r]
            x = w_ref[:, pl.ds(pl.multiple_of(b * LANES, LANES), LANES)].astype(jnp.float32)
            peak = jnp.max(jnp.abs(x), axis=1, keepdims=True)
            scale = (jnp.maximum(peak, floor) / 127.0).astype(jnp.bfloat16).astype(jnp.float32)
            q = (x * (1.0 / scale)).astype(jnp.bfloat16)
            q_ref[r, :, i * LANES:(i + 1) * LANES] = q
            scales = jnp.where(lane == r * group + i, scale, scales)
            acc_ref[pl.ds(b, 1), :] += jnp.sum(q.astype(jnp.float32), axis=0, keepdims=True)
    s_ref[0] = scales.T[:nblocks].astype(jnp.bfloat16)

    @pl.when(step == pl.num_programs(0) - 1)
    def _():
        sums = jnp.sum(acc_ref[...], axis=1, keepdims=True)
        row = lax.broadcasted_iota(jnp.int32, (nblocks, LANES), 0)
        col = lax.broadcasted_iota(jnp.int32, (nblocks, LANES), 1)
        line = jnp.sum(jnp.where(row == col, sums, 0.0), axis=0, keepdims=True)
        p_ref[...] = jnp.broadcast_to(line, p_ref.shape)


def quantize(weight, inv, total_rows):
    rows, cols = weight.shape
    count = inv.shape[0]
    group = cols // LANES // count
    nblocks = count * group
    tile = LANES
    steps = rows // tile
    floor = FLOOR_RATIO / math.sqrt(total_rows)
    return pl.pallas_call(
        functools.partial(quantize_kernel, floor, count, group),
        grid_spec=pltpu.PrefetchScalarGridSpec(
            num_scalar_prefetch=1,
            grid=(steps,),
            in_specs=[pl.BlockSpec((tile, cols), lambda t, inv: (t, 0))],
            out_specs=[
                pl.BlockSpec((count, tile, group * LANES), lambda t, inv: (0, t, 0)),
                pl.BlockSpec((1, nblocks, LANES), lambda t, inv: (t, 0, 0)),
                pl.BlockSpec((8, LANES), lambda t, inv: (0, 0)),
            ],
            scratch_shapes=[pltpu.VMEM((nblocks, LANES), jnp.float32)],
        ),
        out_shape=[
            jax.ShapeDtypeStruct((count, rows, group * LANES), jnp.bfloat16),
            jax.ShapeDtypeStruct((steps, nblocks, LANES), jnp.bfloat16),
            jax.ShapeDtypeStruct((8, LANES), jnp.float32),
        ],
        compiler_params=pltpu.CompilerParams(dimension_semantics=("arbitrary",)),
        cost_estimate=pl.CostEstimate(flops=rows * cols * 8, bytes_accessed=rows * cols * 4, transcendentals=0),
    )(inv, weight)


def flip(m, k):
    bit, out = 1, m
    while bit <= k:
        if k & bit:
            out = out + bit - 2 * bit * ((m // bit) % 2)
        bit *= 2
    return out


def move_kernel(n, count, q_ref, s_ref, p_ref, out_ref, so_ref, po_ref,
                a_send, a_recv, z_send, z_recv, own_sem):
    z = lax.axis_index("dp")
    m = lax.axis_index("mp")
    rows, width = q_ref.shape[1:]
    chunk = rows // CHUNKS
    right, left = (z + 1) % n, (z + n - 1) % n
    near = {1: right, -1: left}
    half = n // 2
    order = sorted(range(1, count), key=lambda k: (bin(k).count("1"), k))

    barrier = pltpu.get_barrier_semaphore()
    for k in range(1, count):
        pl.semaphore_signal(barrier, inc=1, device_id=(z, flip(m, k)), device_id_type=MESH)
    for peer in (right, left):
        pl.semaphore_signal(barrier, inc=1, device_id=(peer, m), device_id_type=MESH)
    pl.semaphore_wait(barrier, count + 1)

    def place(origin, c, src):
        return out_ref.at[pl.ds(pl.multiple_of(origin * rows + c * chunk, 16), chunk),
                          pl.ds(pl.multiple_of(src * width, LANES), width)]

    def plane(unit):
        c, k = unit
        peer = flip(m, k)
        if c < CHUNKS:
            src, dst = q_ref.at[peer, pl.ds(c * chunk, chunk)], place(z, c, m)
        elif c == CHUNKS:
            src, dst = s_ref.at[peer], so_ref.at[z, m]
        else:
            src, dst = p_ref, po_ref.at[z, m]
        return pltpu.make_async_remote_copy(
            src_ref=src, dst_ref=dst, send_sem=a_send.at[c, k - 1], recv_sem=a_recv.at[c, k - 1],
            device_id=(z, peer), device_id_type=MESH)

    def ring(unit, way, hop):
        c, k = unit
        origin = (z + n - way * (hop - 1)) % n
        if c < CHUNKS:
            dst = place(origin, c, flip(m, k))
            src = q_ref.at[m, pl.ds(c * chunk, chunk)] if k == 0 and hop == 1 else dst
        else:
            src = dst = (so_ref if c == CHUNKS else po_ref).at[origin]
        w = 0 if way == 1 else 1
        return pltpu.make_async_remote_copy(
            src_ref=src, dst_ref=dst, send_sem=z_send.at[w, hop - 1, c, k], recv_sem=z_recv.at[w, hop - 1, c, k],
            device_id=(near[way], m), device_id_type=MESH)

    def own(unit):
        c, _ = unit
        if c < CHUNKS:
            src, dst = q_ref.at[m, pl.ds(c * chunk, chunk)], place(z, c, m)
        elif c == CHUNKS:
            src, dst = s_ref.at[m], so_ref.at[z, m]
        else:
            src, dst = p_ref, po_ref.at[z, m]
        return pltpu.make_async_copy(src, dst, own_sem.at[c])

    bulk = [(c, k) for c in range(CHUNKS) for k in [0] + order]
    small = [(CHUNKS, 0), (CHUNKS + 1, 0)]
    units = bulk[:-2] + small + bulk[-2:]
    parity = {unit: j % 2 for j, unit in enumerate(units)}

    def ways(unit, hop):
        if hop < half or n % 2:
            return (1, -1)
        return (1,) if parity[unit] == 0 else (-1,)

    hops = half
    started = []

    def go(copy):
        copy.start()
        started.append(copy)

    for way in ways((0, 0), 1):
        go(ring((0, 0), way, 1))
    for k in order:
        go(plane((0, k)))
    for c in range(1, CHUNKS):
        for way in ways((c, 0), 1):
            go(ring((c, 0), way, 1))
    for c in range(1, CHUNKS + 2):
        for k in order:
            go(plane((c, k)))
    owned = [own((c, 0)) for c in range(CHUNKS + 2)]
    for copy in owned:
        copy.start()

    for unit in units:
        c, k = unit
        if c < CHUNKS and k == 0:
            continue
        if c < CHUNKS:
            plane(unit).wait_recv()
        else:
            owned[c].wait()
            for peer in order:
                plane((c, peer)).wait_recv()
        for way in ways(unit, 1):
            go(ring(unit, way, 1))
    for hop in range(2, hops + 1):
        for unit in units:
            for way in (1, -1):
                if way in ways(unit, hop - 1):
                    if way in ways(unit, hop):
                        ring(unit, way, hop - 1).wait_recv()
                        go(ring(unit, way, hop))
    for hop in range(1, hops + 1):
        for unit in units:
            for way in ways(unit, hop):
                if hop == hops or way not in ways(unit, hop + 1):
                    ring(unit, way, hop).wait_recv()
    for copy in owned[:CHUNKS]:
        copy.wait()
    for copy in started:
        copy.wait_send()


def move(quant, scale, sums, n):
    count, rows, width = quant.shape
    hops = max(n // 2, 1)
    any_spec = pl.BlockSpec(memory_space=pl.ANY)
    dma = pltpu.SemaphoreType.DMA
    sent = rows * width * count * 2 * (n - 1)
    return pl.pallas_call(
        functools.partial(move_kernel, n, count),
        in_specs=[any_spec] * 3,
        out_specs=[any_spec] * 3,
        out_shape=[
            jax.ShapeDtypeStruct((n * rows, count * width), quant.dtype),
            jax.ShapeDtypeStruct((n, count) + scale.shape[1:], scale.dtype),
            jax.ShapeDtypeStruct((n, count) + sums.shape, sums.dtype),
        ],
        scratch_shapes=[
            dma((CHUNKS + 2, count - 1)),
            dma((CHUNKS + 2, count - 1)),
            dma((2, hops, CHUNKS + 2, count)),
            dma((2, hops, CHUNKS + 2, count)),
            dma((CHUNKS + 2,)),
        ],
        compiler_params=pltpu.CompilerParams(collective_id=0, has_side_effects=True),
        cost_estimate=pl.CostEstimate(flops=0, bytes_accessed=sent * 2, transcendentals=0),
    )(quant, scale, sums)


def local(n, weight, rank_map):
    inv = inverse(rank_map)
    rows, cols = weight.shape
    count = rank_map.shape[0]
    group = cols // LANES // count
    nblocks = count * group
    total_rows = rows * n
    quant, scale, sums = quantize(weight, inv, total_rows)
    steps = scale.shape[0]
    scale = scale.reshape(steps, count, group, LANES).transpose(1, 0, 2, 3).reshape(count, steps * group, LANES)
    quant_out, scales, partial_sums = move(quant, scale, sums, n)
    scales = scales.reshape(n, count, steps, group, LANES).transpose(0, 2, 4, 1, 3)
    scale_out = scales.reshape(total_rows, nblocks)
    totals = jnp.sum(partial_sums[:, :, 0, :nblocks], axis=0).reshape(-1)
    return (quant_out, scale_out, totals / (127.0 * math.sqrt(total_rows * LANES)))


def solution(mesh):
    n = mesh.shape["dp"]
    in_specs = (P("dp", "mp"), P())
    out_specs = (P(None, "mp"), P(None, "mp"), P())
    return jax.shard_map(functools.partial(local, n), mesh=mesh, in_specs=in_specs, out_specs=out_specs, check_vma=False)
```

time: 935 us -> 743 us (0.79)
  Pallas kernels: 0 us -> 707 us
  waiting for transfers between devices: 561 us -> 0 us
  blocking collectives: 255 us -> 0 us
  local copies, waits for them, and re-layouts: 69.1 us -> 32.4 us
  other arithmetic: 31.6 us -> 2.21 us
  between operations: 14.1 us -> 0.66 us
    pallas_call x0 -> x2, Pallas kernels: none -> 707 us  [the longest x1 691 us: move(): pl.pallas_call(functools.partial(move_kernel, n, count), in_specs=[any_sp...]
    all_gather x1 -> x0, waiting for transfers between devices: 561 us -> none  [local(): lax.all_gather(local_quant, 'dp', axis=0, tiled=True)]
    all_to_all x1 -> x0, blocking collectives: 123 us -> none  [local(): lax.all_to_all(grouped, 'mp', split_axis=2, concat_axis=1, tiled=True)]
    psum x1 -> x0, blocking collectives: 80.7 us -> none  [local(): totals = lax.psum(whole, ('dp', 'mp'))]
    all_gather x1 -> x0, blocking collectives: 50.5 us -> none  [local(): lax.all_gather(local_scale, 'dp', axis=0, tiled=True)]
    unnamed x5 -> x1, local copies, waits for them, and re-layouts: 44.4 us -> 28.2 us
    reshape x2 -> x3, local copies, waits for them, and re-layouts: 14.4 us -> 3.56 us  [the longest x1 1.53 us: local(): scale.reshape(steps, count, group, LANES).transpose(1, 0, 2, 3)]
    gather x2 -> x0, local copies, waits for them, and re-layouts: 10.1 us -> none  [the longest x1 9.47 us: arrange(): grouped = jnp.take(quant.reshape(rows, group, count, 128), inv, axis=2)]
  transfers between devices with their start and end apart: 2 -> 0, of which waited for: 1 -> 0; matrix products, arithmetic and copies ran while one was open for 1% -> 0% of each run, Pallas kernels for 0% -> 0%
where the time goes in v1:
time: 743 us; the launch traced here: 742 us
  Pallas kernels  707 us (95%)
  local copies, waits for them, and re-layouts  32.4 us (4%)
    pallas_call x1, Pallas kernels, move(): pl.pallas_call(functools.partial(move_kernel, n, count), in_specs=[any_sp...  691 us
    unnamed x1, local copies, waits for them, and re-layouts  28.2 us
    pallas_call x1, Pallas kernels, quantize(): pl.pallas_call(functools.partial(quantize_kernel, floor, count, group), g...  15.8 us

profile of v1, /device:TPU:0, one launch (start us, length us, event | category | flops | bytes accessed | tf_op | source)
XLA Modules:
  0.0 742.3 jit_solution(2289434823456145048)
XLA Ops:
  0.6 1.3 select_reduce_fusion.inv_ref
  1.9 15.8 %shard_map.49 = (bf16[8,1280,512]{2,1,0:T(8,128)(2,1)}, bf16[10,32,128]{2,1,0:T(8,128)(2,1)}, f32[8,128]{1,0:T(8,128)}) custom-call(s32[8]{0:T(128)} %select_reduce_fusion.inv_ref, bf16[1280,4096]{1,0:T(8,128)(2,1)} %w_ref.1), custom_call_target="tpu_custom_call" | custom-call | flops 41943040 | bytes 20971520 | tf_op jit(solution)/shard_map/pallas_call | solution.py:64
  17.7 1.5 copy.9
  19.2 691.3 %shard_map.50 = (bf16[5120,4096]{1,0:T(8,128)(2,1)}, bf16[4,8,40,128]{3,2,1,0:T(8,128)(2,1)}, f32[4,8,8,128]{3,2,1,0:T(8,128)}) custom-call(bf16[8,1280,512]{2,1,0:T(8,128)(2,1)} %get-tuple-element.9.q_ref, bf16[8,40,128]{2,1,0:T(8,128)(2,1)} %bitcast.11, f32[8,128]{1,0:T(8,128)} %get-tuple-element.11.p_ref), custom_call_target="tpu_custom_call" | custom-call | bytes 62914560 | tf_op jit(solution)/shard_map/pallas_call | solution.py:221
  710.5 0.9 slice_reduce_fusion
  711.5 0.6 div.10
  712.1 1.1 copy.12
  713.2 0.9 reshape.25
  714.1 28.2 %copy.14 = bf16[5120,4096]{1,0:T(8,128)(2,1)} copy(bf16[5120,4096]{1,0:T(8,128)(2,1)} %get-tuple-element.18) | data formatting | bytes 83886080
  (1 shorter events, 0.0 us)
